TPU v7x, 32 devices: a whole 2x2x4 slice. The times are simulated.
32 devices in a mesh: samp: 8 (over y, x, core), par: 4 (over z).
Axes of the slice: x: 2, y: 2, z: 4, core: 2. Of those that a mesh axis runs over, the one named last changes fastest.
Arguments:
- log_derivs: bfloat16 [512, 262144], P('samp', 'par')
- energies: float32 [512, 8], P('samp'), may hold values from -6 to 6
- nys_rows: int32 [8, 8], P('samp'), may hold values from 0 to 63, as said below
Outputs:
- update: float32 [262144, 8], P('par')
- solution: float32 [512, 8], P('samp')
Inputs may be any that keep to these rules, and one draw needn't show every extreme that they name: `nys_rows`: each row holds 8 different local sample numbers of that group.
All inputs are finite; a program needn't handle non-finite values.
Results may differ from a plain program's by a relative error of at most 0.014.
Values may be sent and summed in bfloat16 or wider, within the bound.
A program may use at most 128 MiB of HBM per device.

v0:
```python
import math
import jax
import jax.numpy as jnp
from jax import lax
from jax.sharding import PartitionSpec as P

ITERS = 2
damping = 0.5


def factor_solve(factor, right):
    middle = lax.linalg.triangular_solve(factor, right, left_side=True, lower=True)
    return lax.linalg.triangular_solve(factor, middle, left_side=True, lower=True, transpose_a=True)


def small_solve(matrix, right):
    return factor_solve(jnp.linalg.cholesky(matrix), right)


def hdot(left, right):
    return jnp.dot(left, right, precision=lax.Precision.HIGHEST)


def gram_body(log_derivs, energies, nys_rows):
    samp_rows = log_derivs.shape[0]
    groups = lax.axis_size("samp")
    total_rows = samp_rows * groups
    total_cols = log_derivs.shape[1] * lax.axis_size("par")
    slab = lax.all_to_all(log_derivs, "samp", split_axis=1, concat_axis=0, tiled=True)
    widened = slab.astype(jnp.float32)
    col_mean = jnp.sum(widened, axis=0) / total_rows
    centered = ((widened - col_mean) * (1.0 / math.sqrt(total_cols))).astype(jnp.bfloat16)
    gram = lax.psum(
        jnp.einsum("rc,kc->rk", centered, centered, preferred_element_type=jnp.float32),
        ("samp", "par"),
    )
    all_energies = lax.all_gather(energies, "samp", axis=0, tiled=True)
    all_picks = lax.all_gather(nys_rows, "samp", axis=0, tiled=True)
    selected = (jnp.arange(groups, dtype=jnp.int32)[:, None] * samp_rows + all_picks).reshape(-1)
    sketch = jnp.take(gram, selected, axis=1)
    core_block = jnp.take(sketch, selected, axis=0)
    factor = jnp.linalg.cholesky(damping * core_block + hdot(sketch.T, sketch))

    def precondition(residual):
        coeffs = factor_solve(factor, hdot(sketch.T, residual))
        result = (residual - hdot(sketch, coeffs)) / damping
        return (result, hdot(result.T, residual))

    solution = jnp.zeros(all_energies.shape, jnp.float32)
    residual = all_energies
    precond_res, inner_prev = precondition(residual)
    direction = precond_res
    for iteration in range(ITERS):
        rounded = direction.astype(jnp.bfloat16).astype(jnp.float32)
        image_k = hdot(gram, rounded) + damping * direction
        curvature = hdot(direction.T, image_k)
        alpha_k = small_solve(curvature, inner_prev)
        solution = solution + hdot(direction, alpha_k)
        if iteration + 1 < ITERS:
            residual = residual - hdot(image_k, alpha_k)
            precond_res, inner_next = precondition(residual)
            beta_k = small_solve(inner_prev, inner_next)
            direction = precond_res + hdot(direction, beta_k)
            inner_prev = inner_next
    rounded_sol = solution.astype(jnp.bfloat16)
    local_update = jnp.einsum(
        "rc,rv->cv", centered, rounded_sol, preferred_element_type=jnp.float32
    )
    update = lax.all_gather(local_update.astype(jnp.bfloat16), "samp", axis=0, tiled=True).astype(
        local_update.dtype
    )
    start = lax.axis_index("samp") * samp_rows
    return (update, lax.dynamic_slice_in_dim(solution, start, samp_rows, 0))


def body(log_derivs, energies, nys_rows):
    update, solution = gram_body(log_derivs, energies, nys_rows)
    return (update, solution)


def solution(mesh):
    return jax.shard_map(
        body,
        mesh=mesh,
        in_specs=(P("samp", "par"), P("samp", None), P("samp", None)),
        out_specs=(P("par", None), P("samp", None)),
        check_vma=False,
    )
```

profile of v0, /device:TPU:0, one launch (start us, length us, event | category | flops | bytes accessed | tf_op | source)
XLA Modules:
  0.0 351.4 jit_solution(1456690422608163181)
XLA Ops:
  7.2 7.6 %copy.62 = bf16[8,8,8,8192]{3,2,0,1:T(8,128)(2,1)} copy(bf16[8,8,8,8192]{3,2,1,0:T(8,128)(2,1)} %bitcast.122) | data formatting | bytes 16777216 | tf_op jit(solution)/shard_map/all_to_all | solution.py:29
  14.8 5.3 %all-to-all-start = ((bf16[64,8,8192]{2,0,1:T(8,128)(2,1)}), bf16[64,8,8192]{2,0,1:T(8,128)(2,1)}, u32[]{:S(2)}, u32[]{:S(2)}) async-start(bf16[64,8,8192]{2,0,1:T(8,128)(2,1)} %bitcast.121), calls=%async_computation | async-start | bytes 16777216 | tf_op jit(solution)/shard_map/all_to_all | solution.py:29
  20.1 97.4 %all-gather.1 = s32[8,1,8]{2,1,0:T(1,128)S(1)} all-gather(s32[1,1,8]{2,1,0:T(1,128)S(1)} %bitcast.126), channel_id=1, replica_groups=mesh['samp'=8,'par'=4] {'samp'}, dimensions={0}, use_global_device_ids=true | all-gather | bytes 288 | tf_op jit(solution)/shard_map/all_gather | solution.py:38
  117.6 0.1 reshape.104
  117.7 0.1 reshape.103
  117.7 8.3 %all-gather = f32[8,64,8]{1,2,0:T(8,128)S(1)} all-gather(f32[1,64,8]{1,2,0:T(8,128)S(1)} %bitcast.125), channel_id=1, replica_groups=mesh['samp'=8,'par'=4] {'samp'}, dimensions={0}, use_global_device_ids=true | all-gather | bytes 18432 | tf_op jit(solution)/shard_map/all_gather | solution.py:37
  126.0 0.1 reshape.135
  126.1 5.5 %convert_reduce_fusion = f32[8192]{0:T(1024)S(1)} fusion(bf16[64,8,8192]{2,0,1:T(8,128)(2,1)} %all-to-all-done), kind=kLoop, calls=%fused_computation.8 | loop fusion | flops 8380416 | bytes 8421376 | tf_op jit(solution)/shard_map/reduce_sum | solution.py:31
  131.6 8.9 %multiply_convert_fusion = bf16[64,8,8192]{2,0,1:T(8,128)(2,1)} fusion(bf16[64,8,8192]{2,0,1:T(8,128)(2,1)} %all-to-all-done, f32[8192]{0:T(1024)S(1)} %broadcast_multiply_fusion), kind=kLoop, calls=%fused_computation.5 | loop fusion | flops 16777216 | bytes 16809984 | tf_op jit(solution)/shard_map/convert.2
  140.5 11.3 %fusion.73 = f32[512,512]{1,0:T(8,128)} fusion(bf16[512,8192]{1,0:T(8,128)(2,1)} %bitcast.123), kind=kOutput, calls=%fused_computation.118 | convolution fusion | flops 4294967296 | bytes 9437184 | tf_op jit(solution)/shard_map/rc,kc->rk/dot_general | solution.py:34
  151.8 0.2 all-gather.4.cloned.1.call-start
  152.0 8.9 %fusion.1 = bf16[512,8192]{1,0:T(8,128)(2,1)} fusion(bf16[64,8,8192]{2,0,1:T(8,128)(2,1)} %all-to-all-done, f32[8192]{0:T(1024)S(1)} %broadcast_multiply_fusion), kind=kLoop, calls=%fused_computation.4 | loop fusion | flops 16777216 | bytes 16809984 | tf_op jit(solution)/shard_map/convert_element_type | solution.py:32
  160.9 122.7 %all-reduce.2.cloned.1.call-done = f32[512,512]{1,0:T(8,128)} async-done(((f32[512,512]{1,0:T(8,128)}), f32[512,512]{1,0:T(8,128)}) %all-reduce.2.cloned.1.call-update) | async-done | bytes 1048592 | tf_op jit(solution)/shard_map/psum | solution.py:33
  283.6 1.6 copy.48
  285.2 0.7 gather_fusion
  285.9 0.1 select_bitcast_fusion
  286.0 0.1 copy.49
  286.1 0.6 gather_fusion.1
  286.7 0.3 convolution_add_fusion
  287.1 0.1 copy.50
  287.2 5.8 %cholesky.33 = f32[64,64]{1,0:T(8,128)S(1)} custom-call(f32[64,64]{1,0:T(8,128)S(1)} %fusion.29), custom_call_target="Cholesky" | custom-call | tf_op jit(solution)/shard_map/jit(cholesky)/cholesky | solution.py:42
  293.1 0.6 compare_reduce_fusion.3
  293.7 0.7 fusion.20
  294.4 4.9 %custom-call.24 = f32[1,64,64]{1,2,0:T(8,128)S(1)} custom-call(f32[1,64,64]{2,1,0:T(8,128)S(1)} %fusion.20), custom_call_target="InvertDiagBlocksLowerTriangular" | custom-call | tf_op jit(solution)/shard_map/triangular_solve/custom-call.3 | solution.py:13
  299.3 0.3 fusion.7
  299.5 0.2 fusion.25
  299.7 0.2 fusion.27
  299.9 0.3 convolution_subtract_fusion.2
  300.1 0.1 fusion.33
  300.4 1.8 convolution_add_fusion.4
  302.2 0.1 fusion.35
  302.4 0.7 cholesky.94
  303.2 0.6 compare_reduce_fusion.2
  303.8 0.6 fusion.44
  304.5 0.6 custom-call.26
  305.1 0.2 fusion.55
  305.3 0.1 fusion.57
  305.4 0.2 convolution_subtract_fusion.1
  305.6 0.2 fusion.31
  305.9 0.7 cholesky.105
  306.6 0.6 compare_reduce_fusion.1
  307.3 0.6 fusion.45
  307.9 0.6 custom-call.30
  308.5 0.3 fusion.4
  308.8 0.2 fusion.21
  309.0 0.2 fusion.23
  309.1 0.3 fusion.2
  309.4 0.1 fusion.74
  309.6 0.2 fusion.51
  309.8 0.1 fusion.53
  309.9 0.2 convolution_add_fusion.3
  310.1 0.6 convolution_add_fusion.2
  310.7 0.1 fusion.75
  310.9 0.7 cholesky.116
  311.7 0.6 compare_reduce_fusion
  312.4 0.6 fusion.46
  313.0 0.6 custom-call.32
  313.6 0.2 fusion.47
  313.8 0.1 fusion.49
  314.0 0.2 convolution_add_fusion.1
  314.2 5.2 %convolution_convert_fusion = bf16[8192,8]{0,1:T(8,128)(2,1)} fusion(bf16[512,8192]{1,0:T(8,128)(2,1)} %fusion.1, f32[512,8]{0,1:T(8,128)S(1)} %convolution_add_fusion.1), kind=kOutput, calls=%fused_computation.6 | convolution fusion | flops 67178496 | bytes 8536064 | tf_op jit(solution)/shard_map/rc,rv->cv/dot_general | solution.py:66
  319.5 0.7 constant_dynamic-slice_fusion
  320.1 21.8 %all-gather.4.cloned.1.call-done = bf16[65536,8]{0,1:T(8,128)(2,1)} async-done(((bf16[8192,8]{0,1:T(8,128)(2,1)}), bf16[65536,8]{0,1:T(8,128)(2,1)}) %all-gather.4.cloned.1.call-update) | async-done | bytes 1048592 | tf_op jit(solution)/shard_map/all_gather | solution.py:69
  341.9 2.7 convert_element_type.49
  (28 shorter events, 0.7 us)
Async XLA Ops:
  14.8 5.4 %copy-start.2 = (s32[1,8]{1,0:T(1,128)S(1)}, s32[1,8]{1,0:T(1,128)}, u32[]{:S(2)}) copy-start(s32[1,8]{1,0:T(1,128)} %param.14) | copy-start | bytes 100
  14.8 103.0 %copy-start.1 = (f32[64,8]{0,1:T(8,128)S(1)}, f32[64,8]{0,1:T(8,128)}, u32[]{:S(2)}) copy-start(f32[64,8]{0,1:T(8,128)} %param.13) | copy-start | bytes 6148
  14.8 111.4 %all-to-all-start = ((bf16[64,8,8192]{2,0,1:T(8,128)(2,1)}), bf16[64,8,8192]{2,0,1:T(8,128)(2,1)}, u32[]{:S(2)}, u32[]{:S(2)}) async-start(bf16[64,8,8192]{2,0,1:T(8,128)(2,1)} %bitcast.121), calls=%async_computation | async-start | bytes 16777216 | tf_op jit(solution)/shard_map/all_to_all | solution.py:29
  20.1 263.5 %all-reduce.2.cloned.1.call-start = ((), (), s32[]{:S(2)}) async-start(), calls=%async_computation.1 | async-start | bytes 2097152 | tf_op jit(solution)/shard_map/psum | solution.py:33
  151.8 190.1 %all-gather.4.cloned.1.call-start = ((), (), s32[]{:S(2)}) async-start(), calls=%async_computation.2 | async-start | bytes 1179648 | tf_op jit(solution)/shard_map/all_gather | solution.py:69
  283.6 26.5 %copy-start = (f32[512,512]{1,0:T(8,128)S(1)}, f32[512,512]{1,0:T(8,128)}, u32[]{:S(2)}) copy-start(f32[512,512]{1,0:T(8,128)} %all-reduce.2.cloned.1.call-done) | copy-start | bytes 3145732
Sparse Core Ops, SparseCore 0:
  151.9 131.6 all-reduce.1
  319.6 22.3 all-gather.3
where the time goes:
time: 352 us; the launch traced here: 351 us
  waiting for transfers between devices  145 us (41%)
  blocking collectives  106 us (30%)
  other arithmetic  46.2 us (13%)
  matrix products  23.4 us (7%)
  between operations  14.2 us (4%)
  local copies, waits for them, and re-layouts  11.8 us (3%)
  starting transfers between devices  5.59 us (2%)
    psum x1, waiting for transfers between devices, gram_body(): lax.psum(jnp.einsum('rc,kc->rk', centered, centered, preferred_element_ty...  123 us
    all_gather x1, blocking collectives, gram_body(): all_picks = lax.all_gather(nys_rows, 'samp', axis=0, tiled=True)  97.4 us
    all_gather x1, waiting for transfers between devices, gram_body(): lax.all_gather(local_update.astype(jnp.bfloat16), 'samp', axis=0, tiled=T...  21.8 us
    dot_general x1, matrix products, gram_body(): jnp.einsum('rc,kc->rk', centered, centered, preferred_element_type=jnp.fl...  11.3 us
    another operation x8, other arithmetic, factor_solve(): lax.linalg.triangular_solve(factor, middle, left_side=True, lower=True, t...  9.37 us
    another operation x1, other arithmetic  8.89 us
    convert_element_type x1, other arithmetic, gram_body(): ((widened - col_mean) * (1.0 / math.sqrt(total_cols))).astype(jnp.bfloat16)  8.89 us
    all_gather x1, blocking collectives, gram_body(): all_energies = lax.all_gather(energies, 'samp', axis=0, tiled=True)  8.27 us
  transfers between devices with their start and end apart: 3, of which 2 were waited for; matrix products, arithmetic and copies ran while one was open for 3% of the time, Pallas kernels for 0%

commit v1 on v0

--- a/solution.py
+++ b/solution.py
@@ -35,7 +35,12 @@
         ("samp", "par"),
     )
     all_energies = lax.all_gather(energies, "samp", axis=0, tiled=True)
-    all_picks = lax.all_gather(nys_rows, "samp", axis=0, tiled=True)
+    ring = [nys_rows]
+    for hop in range(7):
+        ring.append(lax.ppermute(ring[-1], "samp", [(dev, (dev + 1) % 8) for dev in range(8)]))
+    all_picks = jnp.roll(
+        jnp.concatenate(ring[::-1], axis=0), (lax.axis_index("samp") + 1) * ring[0].shape[0], axis=0
+    )
     selected = (jnp.arange(groups, dtype=jnp.int32)[:, None] * samp_rows + all_picks).reshape(-1)
     sketch = jnp.take(gram, selected, axis=1)
     core_block = jnp.take(sketch, selected, axis=0)

time: 352 us -> 367 us (1.043)
  waiting for transfers between devices: 145 us -> 167 us
  blocking collectives: 106 us -> 97.1 us
    all_gather x1 -> x0, blocking collectives: 97.4 us -> none  [gram_body(): all_picks = lax.all_gather(nys_rows, 'samp', axis=0, tiled=True)]
    all_gather x1, blocking collectives: 8.27 us -> 97.1 us  [gram_body(): all_energies = lax.all_gather(energies, 'samp', axis=0, tiled=True)]
    ppermute x0 -> x7, waiting for transfers between devices: none -> 23 us  [gram_body(): lax.ppermute(ring[-1], 'samp', [(dev, (dev + 1) % 8) for dev in range(8)])]
  transfers between devices with their start and end apart: 3 -> 10, of which waited for: 2 -> 8; matrix products, arithmetic and copies ran while one was open for 3% -> 3% of each run, Pallas kernels for 0% -> 0%
where the time goes in v1:
time: 367 us; the launch traced here: 366 us
  waiting for transfers between devices  167 us (46%)
  blocking collectives  97.1 us (26%)
  other arithmetic  46.2 us (13%)
  matrix products  23.4 us (6%)
  between operations  14.2 us (4%)
  local copies, waits for them, and re-layouts  11.9 us (3%)
  starting transfers between devices  6.48 us (2%)
    psum x1, waiting for transfers between devices, gram_body(): lax.psum(jnp.einsum('rc,kc->rk', centered, centered, preferred_element_ty...  122 us
    all_gather x1, blocking collectives, gram_body(): all_energies = lax.all_gather(energies, 'samp', axis=0, tiled=True)  97.1 us
    ppermute x7, waiting for transfers between devices, gram_body(): lax.ppermute(ring[-1], 'samp', [(dev, (dev + 1) % 8) for dev in range(8)])  23 us
    all_gather x1, waiting for transfers between devices, gram_body(): lax.all_gather(local_update.astype(jnp.bfloat16), 'samp', axis=0, tiled=T...  21.8 us
    dot_general x1, matrix products, gram_body(): jnp.einsum('rc,kc->rk', centered, centered, preferred_element_type=jnp.fl...  11.3 us
    another operation x8, other arithmetic, factor_solve(): lax.linalg.triangular_solve(factor, middle, left_side=True, lower=True, t...  9.37 us
    another operation x1, other arithmetic  8.89 us
    convert_element_type x1, other arithmetic, gram_body(): ((widened - col_mean) * (1.0 / math.sqrt(total_cols))).astype(jnp.bfloat16)  8.89 us
  transfers between devices with their start and end apart: 10, of which 8 were waited for; matrix products, arithmetic and copies ran while one was open for 3% of the time, Pallas kernels for 0%

profile of v1, /device:TPU:0, one launch (start us, length us, event | category | flops | bytes accessed | tf_op | source)
XLA Modules:
  0.0 366.1 jit_solution(11186264684654968957)
XLA Ops:
  7.2 7.6 %copy.62 = bf16[8,8,8,8192]{3,2,0,1:T(8,128)(2,1)} copy(bf16[8,8,8,8192]{3,2,1,0:T(8,128)(2,1)} %bitcast.120) | data formatting | bytes 16777216 | tf_op jit(solution)/shard_map/all_to_all | solution.py:29
  14.8 5.3 %all-to-all-start = ((bf16[64,8,8192]{2,0,1:T(8,128)(2,1)}), bf16[64,8,8192]{2,0,1:T(8,128)(2,1)}, u32[]{:S(2)}, u32[]{:S(2)}) async-start(bf16[64,8,8192]{2,0,1:T(8,128)(2,1)} %bitcast.119), calls=%async_computation | async-start | bytes 16777216 | tf_op jit(solution)/shard_map/all_to_all | solution.py:29
  20.1 0.5 collective-permute-start
  20.7 97.1 %all-gather = f32[8,64,8]{1,2,0:T(8,128)S(1)} all-gather(f32[1,64,8]{1,2,0:T(8,128)S(1)} %bitcast.122), channel_id=1, replica_groups=mesh['samp'=8,'par'=4] {'samp'}, dimensions={0}, use_global_device_ids=true | all-gather | bytes 18432 | tf_op jit(solution)/shard_map/all_gather | solution.py:37
  117.8 0.4 collective-permute-start.1
  118.2 3.5 collective-permute-done.1
  121.8 3.9 %collective-permute-done.2 = s32[1,8]{1,0:T(1,128)S(1)} collective-permute-done((s32[1,8]{1,0:T(1,128)S(1)}, s32[1,8]{1,0:T(1,128)S(1)}, u32[]{:S(2)}, u32[]{:S(2)}) %collective-permute-start.2) | collective-permute-done | bytes 64 | tf_op jit(solution)/shard_map/ppermute | solution.py:40
  125.7 3.9 %collective-permute-done.3 = s32[1,8]{1,0:T(1,128)S(1)} collective-permute-done((s32[1,8]{1,0:T(1,128)S(1)}, s32[1,8]{1,0:T(1,128)S(1)}, u32[]{:S(2)}, u32[]{:S(2)}) %collective-permute-start.3) | collective-permute-done | bytes 64 | tf_op jit(solution)/shard_map/ppermute | solution.py:40
  129.6 3.9 %collective-permute-done.4 = s32[1,8]{1,0:T(1,128)S(1)} collective-permute-done((s32[1,8]{1,0:T(1,128)S(1)}, s32[1,8]{1,0:T(1,128)S(1)}, u32[]{:S(2)}, u32[]{:S(2)}) %collective-permute-start.4) | collective-permute-done | bytes 64 | tf_op jit(solution)/shard_map/ppermute | solution.py:40
  133.4 3.9 %collective-permute-done.5 = s32[1,8]{1,0:T(1,128)S(1)} collective-permute-done((s32[1,8]{1,0:T(1,128)S(1)}, s32[1,8]{1,0:T(1,128)S(1)}, u32[]{:S(2)}, u32[]{:S(2)}) %collective-permute-start.5) | collective-permute-done | bytes 64 | tf_op jit(solution)/shard_map/ppermute | solution.py:40
  137.3 3.9 %collective-permute-done.6 = s32[1,8]{1,0:T(1,128)S(1)} collective-permute-done((s32[1,8]{1,0:T(1,128)S(1)}, s32[1,8]{1,0:T(1,128)S(1)}, u32[]{:S(2)}, u32[]{:S(2)}) %collective-permute-start.6) | collective-permute-done | bytes 64 | tf_op jit(solution)/shard_map/ppermute | solution.py:40
  141.6 5.5 %convert_reduce_fusion = f32[8192]{0:T(1024)S(1)} fusion(bf16[64,8,8192]{2,0,1:T(8,128)(2,1)} %all-to-all-done), kind=kLoop, calls=%fused_computation.8 | loop fusion | flops 8380416 | bytes 8421376 | tf_op jit(solution)/shard_map/reduce_sum | solution.py:31
  147.0 8.9 %multiply_convert_fusion = bf16[64,8,8192]{2,0,1:T(8,128)(2,1)} fusion(bf16[64,8,8192]{2,0,1:T(8,128)(2,1)} %all-to-all-done, f32[8192]{0:T(1024)S(1)} %broadcast_multiply_fusion), kind=kLoop, calls=%fused_computation.5 | loop fusion | flops 16777216 | bytes 16809984 | tf_op jit(solution)/shard_map/convert.2
  155.9 11.3 %fusion.73 = f32[512,512]{1,0:T(8,128)} fusion(bf16[512,8192]{1,0:T(8,128)(2,1)} %bitcast.121), kind=kOutput, calls=%fused_computation.118 | convolution fusion | flops 4294967296 | bytes 9437184 | tf_op jit(solution)/shard_map/rc,kc->rk/dot_general | solution.py:34
  167.2 0.2 all-gather.3.cloned.1.call-start
  167.4 8.9 %fusion.1 = bf16[512,8192]{1,0:T(8,128)(2,1)} fusion(bf16[64,8,8192]{2,0,1:T(8,128)(2,1)} %all-to-all-done, f32[8192]{0:T(1024)S(1)} %broadcast_multiply_fusion), kind=kLoop, calls=%fused_computation.4 | loop fusion | flops 16777216 | bytes 16809984 | tf_op jit(solution)/shard_map/convert_element_type | solution.py:32
  176.3 121.9 %all-reduce.2.cloned.1.call-done = f32[512,512]{1,0:T(8,128)} async-done(((f32[512,512]{1,0:T(8,128)}), f32[512,512]{1,0:T(8,128)}) %all-reduce.2.cloned.1.call-update) | async-done | bytes 1048592 | tf_op jit(solution)/shard_map/psum | solution.py:33
  298.2 1.6 copy.48
  299.9 0.7 gather_fusion
  300.8 0.6 gather_fusion.1
  301.4 0.4 convolution_add_fusion
  301.8 5.8 %cholesky.33 = f32[64,64]{1,0:T(8,128)S(1)} custom-call(f32[64,64]{1,0:T(8,128)S(1)} %fusion.29), custom_call_target="Cholesky" | custom-call | tf_op jit(solution)/shard_map/jit(cholesky)/cholesky | solution.py:47
  307.7 0.6 compare_reduce_fusion.3
  308.3 0.7 fusion.20
  309.0 4.9 %custom-call.24 = f32[1,64,64]{1,2,0:T(8,128)S(1)} custom-call(f32[1,64,64]{2,1,0:T(8,128)S(1)} %fusion.20), custom_call_target="InvertDiagBlocksLowerTriangular" | custom-call | tf_op jit(solution)/shard_map/triangular_solve/custom-call.3 | solution.py:13
  313.9 0.3 fusion.7
  314.2 0.2 fusion.25
  314.4 0.2 fusion.27
  314.5 0.3 convolution_subtract_fusion.2
  314.8 0.1 fusion.33
  315.0 1.8 convolution_add_fusion.4
  316.8 0.1 fusion.35
  317.1 0.7 cholesky.94
  317.8 0.6 compare_reduce_fusion.2
  318.5 0.6 fusion.44
  319.1 0.6 custom-call.26
  319.7 0.2 fusion.55
  319.9 0.1 fusion.57
  320.1 0.2 convolution_subtract_fusion.1
  320.3 0.2 fusion.31
  320.5 0.7 cholesky.105
  321.3 0.6 compare_reduce_fusion.1
  321.9 0.6 fusion.45
  322.6 0.6 custom-call.30
  323.2 0.3 fusion.4
  323.5 0.2 fusion.21
  323.6 0.2 fusion.23
  323.8 0.3 fusion.2
  324.2 0.2 fusion.51
  324.4 0.1 fusion.53
  324.6 0.2 convolution_add_fusion.3
  324.8 0.6 convolution_add_fusion.2
  325.4 0.1 fusion.75
  325.6 0.7 cholesky.116
  326.4 0.6 compare_reduce_fusion
  327.0 0.6 fusion.46
  327.7 0.6 custom-call.32
  328.3 0.2 fusion.47
  328.5 0.1 fusion.49
  328.6 0.2 convolution_add_fusion.1
  328.8 5.2 %convolution_convert_fusion = bf16[8192,8]{0,1:T(8,128)(2,1)} fusion(bf16[512,8192]{1,0:T(8,128)(2,1)} %fusion.1, f32[512,8]{0,1:T(8,128)S(1)} %convolution_add_fusion.1), kind=kOutput, calls=%fused_computation.6 | convolution fusion | flops 67178496 | bytes 8536064 | tf_op jit(solution)/shard_map/rc,rv->cv/dot_general | solution.py:71
  334.1 0.7 constant_dynamic-slice_fusion
  334.8 21.8 %all-gather.3.cloned.1.call-done = bf16[65536,8]{0,1:T(8,128)(2,1)} async-done(((bf16[8192,8]{0,1:T(8,128)(2,1)}), bf16[65536,8]{0,1:T(8,128)(2,1)}) %all-gather.3.cloned.1.call-update) | async-done | bytes 1048592 | tf_op jit(solution)/shard_map/all_gather | solution.py:74
  356.6 2.7 convert_element_type.49
  (42 shorter events, 1.4 us)
Async XLA Ops:
  14.8 5.4 %copy-start.2 = (s32[1,8]{1,0:T(1,128)S(1)}, s32[1,8]{1,0:T(1,128)}, u32[]{:S(2)}) copy-start(s32[1,8]{1,0:T(1,128)} %param.14) | copy-start | bytes 100
  14.8 5.9 %copy-start.1 = (f32[64,8]{0,1:T(8,128)S(1)}, f32[64,8]{0,1:T(8,128)}, u32[]{:S(2)}) copy-start(f32[64,8]{0,1:T(8,128)} %param.13) | copy-start | bytes 6148
  14.8 126.8 %all-to-all-start = ((bf16[64,8,8192]{2,0,1:T(8,128)(2,1)}), bf16[64,8,8192]{2,0,1:T(8,128)(2,1)}, u32[]{:S(2)}, u32[]{:S(2)}) async-start(bf16[64,8,8192]{2,0,1:T(8,128)(2,1)} %bitcast.119), calls=%async_computation | async-start | bytes 16777216 | tf_op jit(solution)/shard_map/all_to_all | solution.py:29
  20.1 278.2 %all-reduce.2.cloned.1.call-start = ((), (), s32[]{:S(2)}) async-start(), calls=%async_computation.1 | async-start | bytes 2097152 | tf_op jit(solution)/shard_map/psum | solution.py:33
  20.1 97.7 %collective-permute-start = (s32[1,8]{1,0:T(1,128)S(1)}, s32[1,8]{1,0:T(1,128)S(1)}, u32[]{:S(2)}, u32[]{:S(2)}) collective-permute-start(s32[1,8]{1,0:T(1,128)S(1)} %copy-done.2), channel_id=1, source_target_pairs={{0,4},{4,8},{8,12},{12,16},{16,20},{20,24},{24,28},{28,0},{1,5},{5... | collective-permute-start | bytes 104 | tf_op jit(solution)/shard_map/ppermute | solution.py:40
  117.8 3.9 %collective-permute-start.1 = (s32[1,8]{1,0:T(1,128)S(1)}, s32[1,8]{1,0:T(1,128)S(1)}, u32[]{:S(2)}, u32[]{:S(2)}) collective-permute-start(s32[1,8]{1,0:T(1,128)S(1)} %collective-permute-done), channel_id=1, source_target_pairs={{0,4},{4,8},{8,12},{12,16},{16,20},{20,24},{24,28},{28,0},{1,5},{5... | collective-permute-start | bytes 104 | tf_op jit(solution)/shard_map/ppermute | solution.py:40
  121.8 3.9 %collective-permute-start.2 = (s32[1,8]{1,0:T(1,128)S(1)}, s32[1,8]{1,0:T(1,128)S(1)}, u32[]{:S(2)}, u32[]{:S(2)}) collective-permute-start(s32[1,8]{1,0:T(1,128)S(1)} %collective-permute-done.1), channel_id=1, source_target_pairs={{0,4},{4,8},{8,12},{12,16},{16,20},{20,24},{24,28},{28,0},{1,5},{5... | collective-permute-start | bytes 104 | tf_op jit(solution)/shard_map/ppermute | solution.py:40
  125.7 3.9 %collective-permute-start.3 = (s32[1,8]{1,0:T(1,128)S(1)}, s32[1,8]{1,0:T(1,128)S(1)}, u32[]{:S(2)}, u32[]{:S(2)}) collective-permute-start(s32[1,8]{1,0:T(1,128)S(1)} %collective-permute-done.2), channel_id=1, source_target_pairs={{0,4},{4,8},{8,12},{12,16},{16,20},{20,24},{24,28},{28,0},{1,5},{5... | collective-permute-start | bytes 104 | tf_op jit(solution)/shard_map/ppermute | solution.py:40
  129.5 3.9 %collective-permute-start.4 = (s32[1,8]{1,0:T(1,128)S(1)}, s32[1,8]{1,0:T(1,128)S(1)}, u32[]{:S(2)}, u32[]{:S(2)}) collective-permute-start(s32[1,8]{1,0:T(1,128)S(1)} %collective-permute-done.3), channel_id=1, source_target_pairs={{0,4},{4,8},{8,12},{12,16},{16,20},{20,24},{24,28},{28,0},{1,5},{5... | collective-permute-start | bytes 104 | tf_op jit(solution)/shard_map/ppermute | solution.py:40
  133.4 3.9 %collective-permute-start.5 = (s32[1,8]{1,0:T(1,128)S(1)}, s32[1,8]{1,0:T(1,128)S(1)}, u32[]{:S(2)}, u32[]{:S(2)}) collective-permute-start(s32[1,8]{1,0:T(1,128)S(1)} %collective-permute-done.4), channel_id=1, source_target_pairs={{0,4},{4,8},{8,12},{12,16},{16,20},{20,24},{24,28},{28,0},{1,5},{5... | collective-permute-start | bytes 104 | tf_op jit(solution)/shard_map/ppermute | solution.py:40
  137.3 3.9 %collective-permute-start.6 = (s32[1,8]{1,0:T(1,128)S(1)}, s32[1,8]{1,0:T(1,128)S(1)}, u32[]{:S(2)}, u32[]{:S(2)}) collective-permute-start(s32[1,8]{1,0:T(1,128)S(1)} %collective-permute-done.5), channel_id=1, source_target_pairs={{0,4},{4,8},{8,12},{12,16},{16,20},{20,24},{24,28},{28,0},{1,5},{5... | collective-permute-start | bytes 104 | tf_op jit(solution)/shard_map/ppermute | solution.py:40
  167.2 189.4 %all-gather.3.cloned.1.call-start = ((), (), s32[]{:S(2)}) async-start(), calls=%async_computation.2 | async-start | bytes 1179648 | tf_op jit(solution)/shard_map/all_gather | solution.py:74
  298.2 26.5 %copy-start = (f32[512,512]{1,0:T(8,128)S(1)}, f32[512,512]{1,0:T(8,128)}, u32[]{:S(2)}) copy-start(f32[512,512]{1,0:T(8,128)} %all-reduce.2.cloned.1.call-done) | copy-start | bytes 3145732
Sparse Core Ops, SparseCore 0:
  167.3 130.8 all-reduce.1
  334.2 22.3 all-gather.2
